TPU v7x, 32 devices: a 4x4x1 block of a 4x4x8 slice. The times are simulated.
32 devices in a mesh: dp: 1 (over z), ep: 32 (over y, x, core).
Axes of the slice: x: 4, y: 4, z: 1, core: 2. Of those that a mesh axis runs over, the one named last changes fastest.
The devices are a block of a 4x4x8 slice.
Arguments:
- tokens_a: bfloat16 [16384, 2048], P(('dp', 'ep'))
- experts_a: int32 [16384, 8], P(('dp', 'ep'))
- slots_a: int32 [16384, 8], P(('dp', 'ep'))
- gates_a: bfloat16 [16384, 8], P(('dp', 'ep'))
- tokens_b: bfloat16 [16384, 2048], P(('dp', 'ep'))
- experts_b: int32 [16384, 8], P(('dp', 'ep'))
- slots_b: int32 [16384, 8], P(('dp', 'ep'))
- gates_b: bfloat16 [16384, 8], P(('dp', 'ep'))
- attn_gain: bfloat16 [2048], replicated
- w_query: bfloat16 [2048, 16, 128], replicated
- w_key: bfloat16 [2048, 16, 128], replicated
- w_value: bfloat16 [2048, 16, 128], replicated
- w_out: bfloat16 [16, 128, 2048], replicated
- moe_gain: bfloat16 [2048], replicated
- w_gate: bfloat16 [64, 2048, 1024], P('ep')
- w_up: bfloat16 [64, 2048, 1024], P('ep')
- w_down: bfloat16 [64, 1024, 2048], P('ep')
Outputs:
- output 1: bfloat16 [16384, 2048], P(('dp', 'ep'))
- output 2: bfloat16 [16384, 2048], P(('dp', 'ep'))
All inputs are finite; a program needn't handle non-finite values.
Results may differ from a plain program's by a relative error of at most 0.0130805.
Values are sent between devices in bfloat16 or wider.
A program may use at most 768 MiB of HBM per device.

v0:
```python
import jax
import jax.numpy as jnp
from jax import lax
from jax.sharding import PartitionSpec as P

NORM_EPS = 1e-6
MASK_VALUE = -1e30


def rms_norm(rows, gain_vec):
    rows_f = rows.astype(jnp.float32)
    inv_rms = lax.rsqrt(jnp.mean(rows_f * rows_f, axis=-1, keepdims=True) + NORM_EPS)
    return (rows_f * inv_rms * gain_vec.astype(jnp.float32)).astype(jnp.bfloat16)


def attention_block(sequence, attn_gain, w_query, w_key, w_value, w_out):
    seq_len = sequence.shape[0]
    normed = rms_norm(sequence, attn_gain)
    query = jnp.einsum("td,dhe->the", normed, w_query, preferred_element_type=jnp.float32).astype(jnp.bfloat16)
    keys = jnp.einsum("td,dhe->the", normed, w_key, preferred_element_type=jnp.float32).astype(jnp.bfloat16)
    values = jnp.einsum("td,dhe->the", normed, w_value, preferred_element_type=jnp.float32).astype(jnp.bfloat16)
    scores = jnp.einsum("qhe,khe->hqk", query, keys, preferred_element_type=jnp.float32) * (w_query.shape[2] ** -0.5)
    causal = lax.broadcasted_iota(jnp.int32, (seq_len, seq_len), 0) >= lax.broadcasted_iota(jnp.int32, (seq_len, seq_len), 1)
    scores = jnp.where(causal[None, :, :], scores, MASK_VALUE)
    attn_prob = jax.nn.softmax(scores, axis=-1).astype(jnp.bfloat16)
    context = jnp.einsum("hqk,khe->qhe", attn_prob, values, preferred_element_type=jnp.float32).astype(jnp.bfloat16)
    attn_out = jnp.einsum("qhe,hed->qd", context, w_out, preferred_element_type=jnp.float32)
    return (sequence.astype(jnp.float32) + attn_out).astype(jnp.bfloat16)


def capacity_of(seq_len, top_k, experts_total):
    return 8 * max(1, (seq_len * top_k) // (4 * experts_total))


def dispatch_rows(normed, dest_row, experts_total, capacity):
    seq_len, model_dim = normed.shape
    top_k = dest_row.shape[0] // seq_len
    token_of = jnp.arange(seq_len * top_k, dtype=jnp.int32) // top_k
    source = jnp.full((experts_total * capacity,), seq_len, jnp.int32).at[dest_row].set(token_of, mode="drop")
    return jnp.take(normed, source, axis=0, mode="fill", fill_value=0).reshape(experts_total, capacity, model_dim)


def combine_rows(residual, returned, dest_row, gates):
    seq_len, model_dim = residual.shape
    top_k = gates.shape[1]
    picked = jnp.take(returned.reshape(-1, model_dim), dest_row, axis=0, mode="fill", fill_value=0).reshape(seq_len, top_k, model_dim)
    mixed_sum = jnp.einsum("tk,tkd->td", gates, picked, preferred_element_type=jnp.float32)
    return (residual.astype(jnp.float32) + mixed_sum).astype(jnp.bfloat16)


def expert_ffn(received, w_gate, w_up, w_down):
    gate_act = jnp.einsum("pecd,edf->pecf", received, w_gate, preferred_element_type=jnp.float32)
    up_act = jnp.einsum("pecd,edf->pecf", received, w_up, preferred_element_type=jnp.float32)
    hidden = (jax.nn.silu(gate_act) * up_act).astype(jnp.bfloat16)
    return jnp.einsum("pecf,efd->pecd", hidden, w_down, preferred_element_type=jnp.float32).astype(jnp.bfloat16)


def moe_layer(tokens, experts, slots, gates, attn_gain, w_query, w_key, w_value, w_out, moe_gain, w_gate, w_up, w_down, group):
    seq_len, model_dim = tokens.shape
    local_experts = w_gate.shape[0]
    experts_total = local_experts * group
    capacity = capacity_of(seq_len, experts.shape[1], experts_total)
    residual = attention_block(tokens, attn_gain, w_query, w_key, w_value, w_out)
    normed = rms_norm(residual, moe_gain)
    dest_row = jnp.where(slots >= 0, experts * capacity + slots, experts_total * capacity).reshape(-1)
    dispatched = dispatch_rows(normed, dest_row, experts_total, capacity)
    received = lax.all_to_all(dispatched, "ep", 0, 0, tiled=True).reshape(group, local_experts, capacity, model_dim)
    expert_out = expert_ffn(received, w_gate, w_up, w_down).reshape(experts_total, capacity, model_dim)
    returned = lax.all_to_all(expert_out, "ep", 0, 0, tiled=True)
    return combine_rows(residual, returned, dest_row, gates)


def solution(mesh):
    group = mesh.shape["ep"]
    row_spec = P(("dp", "ep"), None)
    full_spec = P(None, None, None)
    gain_spec = P(None)
    expert_spec = P("ep", None, None)
    in_specs = (row_spec, row_spec, row_spec, row_spec, row_spec, row_spec, row_spec, row_spec, gain_spec, full_spec, full_spec, full_spec, full_spec, gain_spec, expert_spec, expert_spec, expert_spec)

    def device_fn(tokens_a, experts_a, slots_a, gates_a, tokens_b, experts_b, slots_b, gates_b, attn_gain, w_query, w_key, w_value, w_out, moe_gain, w_gate, w_up, w_down):
        out_a = moe_layer(tokens_a, experts_a, slots_a, gates_a, attn_gain, w_query, w_key, w_value, w_out, moe_gain, w_gate, w_up, w_down, group)
        out_b = moe_layer(tokens_b, experts_b, slots_b, gates_b, attn_gain, w_query, w_key, w_value, w_out, moe_gain, w_gate, w_up, w_down, group)
        return out_a, out_b

    return jax.shard_map(device_fn, mesh=mesh, in_specs=in_specs, out_specs=(row_spec, row_spec), check_vma=False)
```

profile of v0, /device:TPU:107, one launch (start us, length us, event | category | flops | bytes accessed | tf_op | source)
XLA Modules:
  0.0 2226.0 jit_solution(10528022013374989894)
XLA Ops:
  3.7 10.1 fusion.58
  13.8 7.6 fusion.62
  21.9 7.4 fusion.60
  37.3 16.1 scatter_custom_fusion.1
  58.3 12.7 fusion.89
  71.0 17.1 fusion.97
  88.1 17.5 fusion.132
  105.6 18.0 fusion.131
  127.9 14.9 fusion.78
  142.8 15.4 fusion.70
  162.6 63.2 %gather_fusion.2 = bf16[8192,2048]{1,0:T(8,128)(2,1)} fusion(bf16[512,2048]{1,0:T(8,128)(2,1)} %get-tuple-element.4, s32[8192]{0:T(1024)S(1)} %fusion.113), kind=kCustom, calls=%fused_computation.2.clone | custom fusion | bytes 67141632 | tf_op jit(solution)/shard_map/jit(_take)/gather | solution.py:40
  225.8 22.7 %broadcast_select_fusion = bf16[8192,2048]{1,0:T(8,128)(2,1)} fusion(bf16[8192,2048]{1,0:T(8,128)(2,1)} %gather_fusion.2, pred[8192]{0:T(1024)(128)(4,1)S(1)} %copy-done.8), kind=kLoop, calls=%fused_computation.24 | loop fusion | flops 16777216 | bytes 67117056 | tf_op jit(solution)/shard_map/jit(_take)/select_n | solution.py:40
  248.5 7.7 all-to-all-start.2
  256.6 15.7 scatter_custom_fusion
  272.3 40.8 %gather_fusion = bf16[8192,2048]{1,0:T(8,128)(2,1)} fusion(bf16[512,2048]{1,0:T(8,128)(2,1)S(1)} %get-tuple-element.5, s32[8192]{0:T(1024)S(1)} %fusion.112), kind=kCustom, calls=%fused_computation.clone | custom fusion | bytes 67141632 | tf_op jit(solution)/shard_map/jit(_take)/gather | solution.py:40
  313.2 22.7 %broadcast_select_fusion.1 = bf16[8192,2048]{1,0:T(8,128)(2,1)} fusion(bf16[8192,2048]{1,0:T(8,128)(2,1)} %gather_fusion, pred[8192]{0:T(1024)(128)(4,1)S(1)} %compare_and_fusion.1), kind=kLoop, calls=%fused_computation.25 | loop fusion | flops 16777216 | bytes 67117056 | tf_op jit(solution)/shard_map/jit(_take)/select_n | solution.py:40
  335.8 375.8 %all-to-all-done.2 = bf16[64,128,2048]{2,1,0:T(8,128)(2,1)} async-done(((bf16[64,128,2048]{2,1,0:T(8,128)(2,1)}), bf16[64,128,2048]{2,1,0:T(8,128)(2,1)}, u32[]{:S(2)}, u32[]{:S(2)}) %all-to-all-start.2) | async-done | bytes 33554464 | tf_op jit(solution)/shard_map/all_to_all | solution.py:67
  716.5 43.5 %fusion.10 = f32[2,32,128,1024]{3,2,1,0:T(8,128)} fusion(bf16[32,2,128,2048]{3,2,1,0:T(8,128)(2,1)} %bitcast.25, bf16[2,2048,1024]{2,1,0:T(8,128)(2,1)} %param.36), kind=kOutput, calls=%fused_computation.26 | convolution fusion | flops 34359738368 | bytes 75497472 | tf_op jit(solution)/shard_map/pecd,edf->pecf/dot_general | solution.py:53
  760.0 49.1 %fusion.2.clone.4 = bf16[32,2,128,1024]{3,2,0,1:T(8,128)(2,1)} fusion(f32[2,32,128,1024]{3,2,1,0:T(8,128)} %fusion.10, bf16[32,2,128,2048]{3,2,1,0:T(8,128)(2,1)} %bitcast.25, bf16[2,2048,1024]{2,1,0:T(8,128)(2,1)} %param.35), kind=kOutput, calls=%fused_computation.9.clone.clone.clone.1 | convolution fusion | flops 34410070016 | bytes 92274688 | tf_op jit(solution)/shard_map/pecd,edf->pecf/dot_general | solution.py:52
  809.1 43.2 %convert_bitcast_fusion = bf16[32,2,128,2048]{3,2,0,1:T(8,128)(2,1)} fusion(bf16[2,1024,2048]{2,1,0:T(8,128)(2,1)} %param.37, bf16[32,2,128,1024]{3,2,0,1:T(8,128)(2,1)} %fusion.2.clone.4), kind=kOutput, calls=%fused_computation.22 | convolution fusion | flops 34376515584 | bytes 58720256 | tf_op jit(solution)/shard_map/pecf,efd->pecd/dot_general | solution.py:55
  852.3 22.9 %copy.26 = bf16[32,2,128,2048]{3,2,1,0:T(8,128)(2,1)} copy(bf16[32,2,128,2048]{3,2,0,1:T(8,128)(2,1)} %convert_bitcast_fusion) | data formatting | bytes 67108864 | tf_op jit(solution)/shard_map/convert_element_type | solution.py:55
  875.3 295.7 %all-to-all-done = bf16[64,128,2048]{2,1,0:T(8,128)(2,1)} async-done(((bf16[64,128,2048]{2,1,0:T(8,128)(2,1)}), bf16[64,128,2048]{2,1,0:T(8,128)(2,1)}, u32[]{:S(2)}, u32[]{:S(2)}) %all-to-all-start) | async-done | bytes 33554464 | tf_op jit(solution)/shard_map/all_to_all | solution.py:67
  1176.4 43.4 %fusion.14 = f32[2,32,128,1024]{3,2,1,0:T(8,128)} fusion(bf16[32,2,128,2048]{3,2,1,0:T(8,128)(2,1)} %bitcast.5, bf16[2,2048,1024]{2,1,0:T(8,128)(2,1)} %param.36), kind=kOutput, calls=%fused_computation.30 | convolution fusion | flops 34359738368 | bytes 75497472 | tf_op jit(solution)/shard_map/pecd,edf->pecf/dot_general | solution.py:53
  1219.9 49.4 %fusion.6.clone.2 = bf16[32,2,128,1024]{3,2,0,1:T(8,128)(2,1)} fusion(f32[2,32,128,1024]{3,2,1,0:T(8,128)} %fusion.14, bf16[32,2,128,2048]{3,2,1,0:T(8,128)(2,1)} %bitcast.5, bf16[2,2048,1024]{2,1,0:T(8,128)(2,1)} %param.35), kind=kOutput, calls=%fused_computation.16.clone.clone.clone | convolution fusion | flops 34410070016 | bytes 92274688 | tf_op jit(solution)/shard_map/pecd,edf->pecf/dot_general | solution.py:52
  1269.2 43.2 %convert_bitcast_fusion.1 = bf16[32,2,128,2048]{3,2,0,1:T(8,128)(2,1)} fusion(bf16[2,1024,2048]{2,1,0:T(8,128)(2,1)} %param.37, bf16[32,2,128,1024]{3,2,0,1:T(8,128)(2,1)} %fusion.6.clone.2), kind=kOutput, calls=%fused_computation.23 | convolution fusion | flops 34376515584 | bytes 58720256 | tf_op jit(solution)/shard_map/pecf,efd->pecd/dot_general | solution.py:55
  1312.4 22.9 %copy.22 = bf16[32,2,128,2048]{3,2,1,0:T(8,128)(2,1)} copy(bf16[32,2,128,2048]{3,2,0,1:T(8,128)(2,1)} %convert_bitcast_fusion.1) | data formatting | bytes 67108864 | tf_op jit(solution)/shard_map/convert_element_type | solution.py:55
  1335.4 295.6 %all-to-all-done.3 = bf16[64,128,2048]{2,1,0:T(8,128)(2,1)} async-done(((bf16[64,128,2048]{2,1,0:T(8,128)(2,1)}), bf16[64,128,2048]{2,1,0:T(8,128)(2,1)}, u32[]{:S(2)}, u32[]{:S(2)}) %all-to-all-start.3) | async-done | bytes 33554464 | tf_op jit(solution)/shard_map/all_to_all | solution.py:69
  1636.9 120.3 %gather_fusion.3 = bf16[4096,2048]{1,0:T(8,128)(2,1)} fusion(bf16[8192,2048]{1,0:T(8,128)(2,1)} %bitcast.33, s32[4096]{0:T(1024)S(1)} %fusion.122), kind=kCustom, calls=%fused_computation.3.clone | custom fusion | bytes 33570816 | tf_op jit(solution)/shard_map/jit(_take)/gather | solution.py:46
  1757.3 8.8 fusion.22
  1769.0 321.8 %all-to-all-done.1 = bf16[64,128,2048]{2,1,0:T(8,128)(2,1)} async-done(((bf16[64,128,2048]{2,1,0:T(8,128)(2,1)}), bf16[64,128,2048]{2,1,0:T(8,128)(2,1)}, u32[]{:S(2)}, u32[]{:S(2)}) %all-to-all-start.1) | async-done | bytes 33554464 | tf_op jit(solution)/shard_map/all_to_all | solution.py:69
  2090.8 123.4 %gather_fusion.1 = bf16[4096,2048]{1,0:T(8,128)(2,1)} fusion(bf16[8192,2048]{1,0:T(8,128)(2,1)} %bitcast.16, s32[4096]{0:T(1024)S(1)} %fusion.121), kind=kCustom, calls=%fused_computation.1.clone | custom fusion | bytes 33570816 | tf_op jit(solution)/shard_map/jit(_take)/gather | solution.py:46
  2214.1 8.8 fusion.24
  (82 shorter events, 47.4 us)
Async XLA Ops:
  1.4 12.3 slice-start.2
  3.6 10.1 copy-start.6
  3.7 10.1 slice-start.3
  3.7 18.2 slice-start
  13.8 7.6 copy-start.7
  13.8 8.1 slice-start.1
  29.3 7.4 copy-start.9
  29.3 7.4 copy-start.10
  36.7 0.6 copy-start.13
  36.9 34.1 %copy-start.2 = (s32[512,8]{1,0:T(8,128)}, s32[512,8]{1,0:T(8,128)S(1)}, u32[]{:S(2)}) copy-start(s32[512,8]{1,0:T(8,128)S(1)} %copy.23) | copy-start | bytes 49156
  105.6 22.2 copy-start.16
  162.6 63.2 %copy-start.8 = (pred[8192]{0:T(1024)(128)(4,1)S(1)}, pred[8192]{0:T(1024)(128)(4,1)}, u32[]{:S(2)}) copy-start(pred[8192]{0:T(1024)(128)(4,1)} %compare_and_fusion) | copy-start | bytes 24580
  248.5 7.7 copy-start.11
  248.5 7.7 copy-start.12
  248.5 463.2 %all-to-all-start.2 = ((bf16[64,128,2048]{2,1,0:T(8,128)(2,1)}), bf16[64,128,2048]{2,1,0:T(8,128)(2,1)}, u32[]{:S(2)}, u32[]{:S(2)}) async-start(bf16[64,128,2048]{2,1,0:T(8,128)(2,1)} %bitcast.140), calls=%async_computation.2 | async-start | bytes 67108864 | tf_op jit(solution)/shard_map/all_to_all | solution.py:67
  256.4 56.8 %copy-start.4 = (s32[512,8]{1,0:T(8,128)}, s32[512,8]{1,0:T(8,128)S(1)}, u32[]{:S(2)}) copy-start(s32[512,8]{1,0:T(8,128)S(1)} %copy.19) | copy-start | bytes 49156
  711.6 459.3 %all-to-all-start = ((bf16[64,128,2048]{2,1,0:T(8,128)(2,1)}), bf16[64,128,2048]{2,1,0:T(8,128)(2,1)}, u32[]{:S(2)}, u32[]{:S(2)}) async-start(bf16[64,128,2048]{2,1,0:T(8,128)(2,1)} %bitcast.141), calls=%async_computation | async-start | bytes 67108864 | tf_op jit(solution)/shard_map/all_to_all | solution.py:67
  1171.0 460.0 %all-to-all-start.3 = ((bf16[64,128,2048]{2,1,0:T(8,128)(2,1)}), bf16[64,128,2048]{2,1,0:T(8,128)(2,1)}, u32[]{:S(2)}, u32[]{:S(2)}) async-start(bf16[64,128,2048]{2,1,0:T(8,128)(2,1)} %bitcast.142), calls=%async_computation.3 | async-start | bytes 67108864 | tf_op jit(solution)/shard_map/all_to_all | solution.py:69
  1631.0 5.2 copy-start.3
  1631.0 5.4 copy-start.5
  1631.0 5.5 copy-start.14
  1631.0 5.7 copy-start.15
  1631.0 459.8 %all-to-all-start.1 = ((bf16[64,128,2048]{2,1,0:T(8,128)(2,1)}), bf16[64,128,2048]{2,1,0:T(8,128)(2,1)}, u32[]{:S(2)}, u32[]{:S(2)}) async-start(bf16[64,128,2048]{2,1,0:T(8,128)(2,1)} %bitcast.139), calls=%async_computation.1 | async-start | bytes 67108864 | tf_op jit(solution)/shard_map/all_to_all | solution.py:69
  1757.3 8.8 copy-start.1
  2214.1 8.8 copy-start
where the time goes:
time: 2230 us
  waiting for transfers between devices  1290 us (58%)
  local copies, waits for them, and re-layouts  435 us (20%)
  matrix products  382 us (17%)
  other arithmetic  95.3 us (4%)
  starting transfers between devices  23.2 us (1%)
    all_to_all x2, waiting for transfers between devices, moe_layer(): lax.all_to_all(dispatched, 'ep', 0, 0, tiled=True)  672 us
    all_to_all x2, waiting for transfers between devices, moe_layer(): returned = lax.all_to_all(expert_out, 'ep', 0, 0, tiled=True)  617 us
    gather x2, local copies, waits for them, and re-layouts, combine_rows(): jnp.take(returned.reshape(-1, model_dim), dest_row, axis=0, mode='fill',...  244 us
    gather x2, local copies, waits for them, and re-layouts, dispatch_rows(): jnp.take(normed, source, axis=0, mode='fill', fill_value=0)  104 us
    dot_general x2, matrix products, expert_ffn(): jnp.einsum('pecd,edf->pecf', received, w_gate, preferred_element_type=jnp...  98.5 us
    dot_general x2, matrix products, expert_ffn(): jnp.einsum('pecd,edf->pecf', received, w_up, preferred_element_type=jnp.f...  86.9 us
    dot_general x2, matrix products, expert_ffn(): jnp.einsum('pecf,efd->pecd', hidden, w_down, preferred_element_type=jnp.f...  86.4 us
    convert_element_type x2, local copies, waits for them, and re-layouts, expert_ffn(): jnp.einsum('pecf,efd->pecd', hidden, w_down, preferred_element_type=jnp.f...  45.8 us
  transfers between devices with their start and end apart: 4, of which 4 were waited for; matrix products, arithmetic and copies ran while one was open for 24% of the time, Pallas kernels for 0%

commit v1 on v0

v1 whole, which is shorter than its diff:
```python
import functools

import jax
import jax.numpy as jnp
from jax import lax
from jax.experimental import pallas as pl
from jax.experimental.pallas import tpu as pltpu
from jax.sharding import PartitionSpec as P

NORM_EPS = 1e-6
MASK_VALUE = -1e30
MESH = pl.DeviceIdType.MESH
VMEM_LIMIT = 64_000_000


def rms_norm(rows, gain_vec):
    rows_f = rows.astype(jnp.float32)
    inv_rms = lax.rsqrt(jnp.mean(rows_f * rows_f, axis=-1, keepdims=True) + NORM_EPS)
    return (rows_f * inv_rms * gain_vec.astype(jnp.float32)).astype(jnp.bfloat16)


def attention_block(sequence, attn_gain, w_query, w_key, w_value, w_out):
    seq_len = sequence.shape[0]
    normed = rms_norm(sequence, attn_gain)
    query = jnp.einsum("td,dhe->the", normed, w_query, preferred_element_type=jnp.float32).astype(jnp.bfloat16)
    keys = jnp.einsum("td,dhe->the", normed, w_key, preferred_element_type=jnp.float32).astype(jnp.bfloat16)
    values = jnp.einsum("td,dhe->the", normed, w_value, preferred_element_type=jnp.float32).astype(jnp.bfloat16)
    scores = jnp.einsum("qhe,khe->hqk", query, keys, preferred_element_type=jnp.float32) * (w_query.shape[2] ** -0.5)
    causal = lax.broadcasted_iota(jnp.int32, (seq_len, seq_len), 0) >= lax.broadcasted_iota(jnp.int32, (seq_len, seq_len), 1)
    scores = jnp.where(causal[None, :, :], scores, MASK_VALUE)
    attn_prob = jax.nn.softmax(scores, axis=-1).astype(jnp.bfloat16)
    context = jnp.einsum("hqk,khe->qhe", attn_prob, values, preferred_element_type=jnp.float32).astype(jnp.bfloat16)
    attn_out = jnp.einsum("qhe,hed->qd", context, w_out, preferred_element_type=jnp.float32)
    return (sequence.astype(jnp.float32) + attn_out).astype(jnp.bfloat16)


def capacity_of(seq_len, top_k, experts_total):
    return 8 * max(1, (seq_len * top_k) // (4 * experts_total))


def place(group):
    side = int(round((group // 2) ** 0.5))
    me = lax.axis_index("ep")
    return side, lax.rem(me // 2, side), me // (2 * side), lax.rem(me, 2)


def expert_kernel(group, cap, u_hbm, after_hbm, dest_ref, wg_hbm, wu_hbm, wd_hbm, ret_hbm, wg_v, wu_v, wd_v, u_buf, x_buf, h_buf, o_buf, w_sem, u_sem, send_sem, recv_sem):
    local_experts, model_dim, ffn_dim = wg_v.shape
    per_step, seq_len, _ = u_buf.shape
    top_k = dest_ref.shape[1]
    block_rows = local_experts * cap
    half_dim = model_dim // 2
    steps = group // per_step
    f_tile = min(512, ffn_dim)
    n_tile = min(512, half_dim)
    side, my_x, my_y, my_core = place(group)
    line = 2 * side
    me = my_y * line + my_x * 2 + my_core
    mine = (my_y * 2 + my_core, my_x * 2 + my_core)

    def target(step, g):
        late = step // side
        i = lax.rem(step, side)
        if g < 2:
            dx, dy = i, 1 - late
        else:
            dx, dy = (1 - late) * (side - i) + late * (i + 2), 3 - late
        return lax.rem(my_x + dx, side), lax.rem(my_y + dy, side), g % 2

    def load(step, g):
        to_x, to_y, core = target(step, g)
        start = pl.multiple_of((to_y * line + to_x * 2 + core) * seq_len, seq_len)
        return pltpu.make_async_copy(u_hbm.at[pl.ds(start, seq_len)], u_buf.at[g], u_sem.at[g])

    def relay(step, g, half):
        to_x, to_y, core = target(step, g)
        return to_y * line + my_x * 2 + core if half == 0 else my_y * line + to_x * 2 + core

    def landing(step, g, half):
        to_x, to_y, _ = target(step, g)
        return ret_hbm.at[half, to_y if half else to_x, mine[half]]

    def send(step, g, half, slot):
        to_x, to_y, _ = target(step, g)
        return pltpu.make_async_remote_copy(
            src_ref=o_buf.at[slot, half, g],
            dst_ref=landing(step, g, half),
            send_sem=send_sem.at[slot, half, g],
            recv_sem=recv_sem.at[half, to_y if half else to_x, mine[half]],
            device_id={"ep": relay(step, g, half)},
            device_id_type=MESH,
        )

    def keep(step, g, half, slot):
        return pltpu.make_async_copy(o_buf.at[slot, half, g], landing(step, g, half), send_sem.at[slot, half, g])

    def start_out(step, slot):
        for g in range(per_step):
            for half in range(2):

                @pl.when(relay(step, g, half) == me)
                def _():
                    keep(step, g, half, slot).start()

                @pl.when(relay(step, g, half) != me)
                def _():
                    send(step, g, half, slot).start()

    def wait_out(step, slot):
        for g in range(per_step):
            for half in range(2):

                @pl.when(relay(step, g, half) == me)
                def _():
                    keep(step, g, half, slot).wait()

                @pl.when(relay(step, g, half) != me)
                def _():
                    send(step, g, half, slot).wait_send()

    weights = [pltpu.make_async_copy(a, b, w_sem.at[i]) for i, (a, b) in enumerate(((wg_hbm, wg_v), (wu_hbm, wu_v), (wd_hbm, wd_v)))]
    for g in range(per_step):
        load(0, g).start()
    for w in weights:
        w.start()

    barrier = pltpu.get_barrier_semaphore()

    @pl.loop(1, line)
    def _(k):
        j = lax.rem(mine[0] + k, line)
        pl.semaphore_signal(barrier, inc=1, device_id={"ep": (j // 2) * line + my_x * 2 + lax.rem(j, 2)}, device_id_type=MESH)
        j = lax.rem(mine[1] + k, line)
        pl.semaphore_signal(barrier, inc=1, device_id={"ep": my_y * line + j}, device_id_type=MESH)

    pl.semaphore_wait(barrier, 2 * (line - 1))
    for w in weights:
        w.wait()

    row_id = (me * block_rows + lax.broadcasted_iota(jnp.int32, (block_rows, seq_len), 0)).astype(jnp.float32)

    @pl.loop(0, steps)
    def _(step):
        slot = lax.rem(step, 2)
        for g in range(per_step):
            load(step, g).wait()
            to_x, to_y, core = target(step, g)
            dest = dest_ref[to_y * line + to_x * 2 + core]
            hit = row_id == dest[0:1, :]
            for j in range(1, top_k):
                hit = hit | (row_id == dest[j : j + 1, :])
            pick = jnp.where(hit, 1.0, 0.0).astype(jnp.bfloat16)
            for n in range(model_dim // n_tile):
                cols = slice(n * n_tile, (n + 1) * n_tile)
                rows = jnp.dot(pick, u_buf[g, :, cols], preferred_element_type=jnp.float32).astype(jnp.bfloat16)
                for e in range(local_experts):
                    x_buf[e, g * cap : (g + 1) * cap, cols] = rows[e * cap : (e + 1) * cap]

            @pl.when(step < steps - 1)
            def _():
                load(step + 1, g).start()

        @pl.when(step >= 2)
        def _():
            wait_out(step - 2, slot)

        for e in range(local_experts):

            @pl.loop(0, ffn_dim // f_tile)
            def _(f):
                cols = pl.ds(pl.multiple_of(f * f_tile, f_tile), f_tile)
                gate_act = jnp.dot(x_buf[e], wg_v[e, :, cols], preferred_element_type=jnp.float32)
                up_act = jnp.dot(x_buf[e], wu_v[e, :, cols], preferred_element_type=jnp.float32)
                h_buf[:, cols] = (gate_act * jax.nn.sigmoid(gate_act) * up_act).astype(jnp.bfloat16)

            for half in range(2):

                @pl.loop(0, half_dim // n_tile)
                def _(n):
                    cols = pl.ds(pl.multiple_of(n * n_tile, n_tile), n_tile)
                    w_cols = pl.ds(pl.multiple_of(half * half_dim + n * n_tile, n_tile), n_tile)
                    rows = jnp.dot(h_buf[...], wd_v[e, :, w_cols], preferred_element_type=jnp.float32).astype(jnp.bfloat16)
                    for g in range(per_step):
                        o_buf[slot, half, g, e * cap : (e + 1) * cap, cols] = rows[g * cap : (g + 1) * cap]

        start_out(step, slot)

    for step in range(max(0, steps - 2), steps):
        wait_out(step, step % 2)

    @pl.loop(1, line)
    def _(k):
        for half in range(2):
            j = lax.rem(mine[half] + k, line)
            peer = (j // 2) * line + my_x * 2 + lax.rem(j, 2) if half == 0 else my_y * line + j
            for t in range(side):
                pltpu.make_async_remote_copy(
                    src_ref=o_buf.at[0, half, 0],
                    dst_ref=ret_hbm.at[half, t, j],
                    send_sem=send_sem.at[0, half, 0],
                    recv_sem=recv_sem.at[half, t, j],
                    device_id={"ep": peer},
                    device_id_type=MESH,
                ).wait_recv()


def experts_to_relays(gathered, after, dest_all, w_gate, w_up, w_down, group, cap):
    local_experts, model_dim, ffn_dim = w_gate.shape
    seq_len = gathered.shape[0] // group
    side = int(round((group // 2) ** 0.5))
    per_step = 4
    rows = group * local_experts * cap
    hbm = pl.BlockSpec(memory_space=pl.ANY)
    return pl.pallas_call(
        functools.partial(expert_kernel, group, cap),
        out_shape=jax.ShapeDtypeStruct((2, side, 2 * side, local_experts * cap, model_dim // 2), jnp.bfloat16),
        in_specs=[hbm, hbm, pl.BlockSpec(memory_space=pltpu.VMEM), hbm, hbm, hbm],
        out_specs=hbm,
        scratch_shapes=[
            pltpu.VMEM(w_gate.shape, jnp.bfloat16),
            pltpu.VMEM(w_up.shape, jnp.bfloat16),
            pltpu.VMEM(w_down.shape, jnp.bfloat16),
            pltpu.VMEM((per_step, seq_len, model_dim), jnp.bfloat16),
            pltpu.VMEM((local_experts, per_step * cap, model_dim), jnp.bfloat16),
            pltpu.VMEM((per_step * cap, ffn_dim), jnp.bfloat16),
            pltpu.VMEM((2, 2, per_step, local_experts * cap, model_dim // 2), jnp.bfloat16),
            pltpu.SemaphoreType.DMA((3,)),
            pltpu.SemaphoreType.DMA((per_step,)),
            pltpu.SemaphoreType.DMA((2, 2, per_step)),
            pltpu.SemaphoreType.DMA((2, side, 2 * side)),
        ],
        compiler_params=pltpu.CompilerParams(collective_id=0, has_side_effects=True, vmem_limit_bytes=VMEM_LIMIT),
        cost_estimate=pl.CostEstimate(flops=2 * rows * model_dim * (3 * ffn_dim + seq_len), bytes_accessed=200_000_000, transcendentals=0),
        name="experts_to_relays",
    )(gathered, after, dest_all, w_gate, w_up, w_down)


def relay_kernel(group, ret_hbm, dest_ref, gates_ref, part_hbm, r_buf, w_buf, p_buf, r_sem, send_sem, recv_sem):
    side, my_x, my_y, my_core = place(group)
    line = 2 * side
    _, block_rows, half_dim = r_buf.shape[1:]
    n_tile = min(512, half_dim)
    mine = (my_x, my_y)

    def target(i, half):
        return lax.rem(mine[half] + side - 1 - i, side)

    def device(half, t):
        return my_y * line + t * 2 + my_core if half == 0 else t * line + my_x * 2 + my_core

    def load(i, half):
        return pltpu.make_async_copy(ret_hbm.at[half, target(i, half)], r_buf.at[half], r_sem.at[half])

    def send(i, half):
        return pltpu.make_async_remote_copy(
            src_ref=p_buf.at[i, half],
            dst_ref=part_hbm.at[half, mine[half]],
            send_sem=send_sem.at[i, half],
            recv_sem=recv_sem.at[half, mine[half]],
            device_id={"ep": device(half, target(i, half))},
            device_id_type=MESH,
        )

    def keep(half):
        return pltpu.make_async_copy(p_buf.at[side - 1, half], part_hbm.at[half, mine[half]], send_sem.at[side - 1, half])

    for half in range(2):
        load(0, half).start()

    barrier = pltpu.get_barrier_semaphore()
    for half in range(2):
        for k in range(1, side):
            pl.semaphore_signal(barrier, inc=1, device_id={"ep": device(half, lax.rem(mine[half] + k, side))}, device_id_type=MESH)
    pl.semaphore_wait(barrier, 2 * (side - 1))

    seq_len, top_k = dest_ref.shape[1:]
    lane = lax.broadcasted_iota(jnp.int32, (seq_len, block_rows), 1)

    @pl.loop(0, side)
    def _(i):
        for half in range(2):
            t = target(i, half)
            dest = dest_ref[half * side + t]
            gates = gates_ref[half * side + t]
            for j in range(line):
                owner = (j // 2) * line + my_x * 2 + j % 2 if half == 0 else my_y * line + j
                row_id = (owner * block_rows + lane).astype(jnp.float32)
                mix = jnp.zeros((seq_len, block_rows), jnp.float32)
                for k in range(top_k):
                    mix = jnp.where(dest[:, k : k + 1] == row_id, gates[:, k : k + 1], mix)
                w_buf[:, j * block_rows : (j + 1) * block_rows] = mix.astype(jnp.bfloat16)
            load(i, half).wait()
            for n in range(half_dim // n_tile):
                cols = slice(n * n_tile, (n + 1) * n_tile)
                rows = r_buf[half, :, :, cols].reshape(line * block_rows, n_tile)
                p_buf[i, half, :, cols] = jnp.dot(w_buf[...], rows, preferred_element_type=jnp.float32)

            @pl.when(i < side - 1)
            def _():
                load(i + 1, half).start()
                send(i, half).start()

            @pl.when(i == side - 1)
            def _():
                keep(half).start()

    for half in range(2):
        keep(half).wait()
        for i in range(side - 1):
            send(i, half).wait_send()
        for k in range(1, side):
            j = lax.rem(mine[half] + k, side)
            pltpu.make_async_remote_copy(
                src_ref=p_buf.at[0, half],
                dst_ref=part_hbm.at[half, j],
                send_sem=send_sem.at[0, half],
                recv_sem=recv_sem.at[half, j],
                device_id={"ep": device(half, j)},
                device_id_type=MESH,
            ).wait_recv()


def relay_sums(ret, dest, gates, group):
    _, side, line, block_rows, half_dim = ret.shape
    seq_len = dest.shape[1]
    hbm = pl.BlockSpec(memory_space=pl.ANY)
    vmem = pl.BlockSpec(memory_space=pltpu.VMEM)
    return pl.pallas_call(
        functools.partial(relay_kernel, group),
        out_shape=jax.ShapeDtypeStruct((2, side, seq_len, half_dim), jnp.float32),
        in_specs=[hbm, vmem, vmem],
        out_specs=hbm,
        scratch_shapes=[
            pltpu.VMEM((2, line, block_rows, half_dim), jnp.bfloat16),
            pltpu.VMEM((seq_len, line * block_rows), jnp.bfloat16),
            pltpu.VMEM((side, 2, seq_len, half_dim), jnp.float32),
            pltpu.SemaphoreType.DMA((2,)),
            pltpu.SemaphoreType.DMA((side, 2)),
            pltpu.SemaphoreType.DMA((2, side)),
        ],
        compiler_params=pltpu.CompilerParams(collective_id=1, has_side_effects=True, vmem_limit_bytes=VMEM_LIMIT),
        cost_estimate=pl.CostEstimate(flops=2 * seq_len * ret.size, bytes_accessed=2 * ret.size + 8 * side * seq_len * half_dim, transcendentals=0),
        name="relay_sums",
    )(ret, dest, gates)


def final_kernel(resid_ref, part_ref, out_ref):
    total = resid_ref[...].astype(jnp.float32)
    for i in range(part_ref.shape[1]):
        total = total + part_ref[0, i]
    out_ref[...] = total.astype(out_ref.dtype)


def final_sum(residual, part):
    seq_len, model_dim = residual.shape
    side, half_dim = part.shape[1], part.shape[3]
    tile = min(128, seq_len)
    return pl.pallas_call(
        final_kernel,
        grid=(2, seq_len // tile),
        out_shape=jax.ShapeDtypeStruct(residual.shape, residual.dtype),
        in_specs=[pl.BlockSpec((tile, half_dim), lambda h, r: (r, h)), pl.BlockSpec((1, side, tile, half_dim), lambda h, r: (h, 0, r, 0))],
        out_specs=pl.BlockSpec((tile, half_dim), lambda h, r: (r, h)),
        cost_estimate=pl.CostEstimate(flops=part.size, bytes_accessed=4 * part.size + 4 * residual.size, transcendentals=0),
        name="final_sum",
    )(residual, part)


def solution(mesh):
    group = mesh.shape["ep"]
    row_spec = P(("dp", "ep"), None)
    full_spec = P(None, None, None)
    gain_spec = P(None)
    expert_spec = P("ep", None, None)
    in_specs = (row_spec, row_spec, row_spec, row_spec, row_spec, row_spec, row_spec, row_spec, gain_spec, full_spec, full_spec, full_spec, full_spec, gain_spec, expert_spec, expert_spec, expert_spec)

    def device_fn(tokens_a, experts_a, slots_a, gates_a, tokens_b, experts_b, slots_b, gates_b, attn_gain, w_query, w_key, w_value, w_out, moe_gain, w_gate, w_up, w_down):
        seq_len, top_k = experts_a.shape
        cap = capacity_of(seq_len, top_k, w_gate.shape[0] * group)
        dest_a = jnp.where(slots_a >= 0, experts_a * cap + slots_a, -1)
        dest_b = jnp.where(slots_b >= 0, experts_b * cap + slots_b, -1)
        table = jnp.stack([v.T.astype(jnp.float32) for v in (dest_a, gates_a, dest_b, gates_b)])
        table = lax.all_gather(table, "ep")
        side, my_x, my_y, my_core = place(group)
        grid = table.reshape((side, side, 2) + table.shape[1:])
        grid = lax.dynamic_index_in_dim(grid, my_core, 2, keepdims=False)
        lines = jnp.concatenate([lax.dynamic_index_in_dim(grid, my_y, 0, keepdims=False), lax.dynamic_index_in_dim(grid, my_x, 1, keepdims=False)])
        lines = jnp.swapaxes(lines, 2, 3)

        resid_a = attention_block(tokens_a, attn_gain, w_query, w_key, w_value, w_out)
        normed_a = rms_norm(resid_a, moe_gain)
        gathered_a = lax.all_gather(normed_a, "ep", tiled=True)
        tokens_b, normed_a = lax.optimization_barrier((tokens_b, normed_a))
        resid_b = attention_block(tokens_b, attn_gain, w_query, w_key, w_value, w_out)
        normed_b = rms_norm(resid_b, moe_gain)
        gathered_b = lax.all_gather(normed_b, "ep", tiled=True)

        returned_a = experts_to_relays(gathered_a, normed_b, table[:, 0], w_gate, w_up, w_down, group, cap)
        part_a = relay_sums(returned_a, lines[:, 0], lines[:, 1], group)
        out_a = final_sum(resid_a, part_a)
        returned_b = experts_to_relays(gathered_b, out_a, table[:, 2], w_gate, w_up, w_down, group, cap)
        part_b = relay_sums(returned_b, lines[:, 2], lines[:, 3], group)
        return out_a, final_sum(resid_b, part_b)

    return jax.shard_map(device_fn, mesh=mesh, in_specs=in_specs, out_specs=(row_spec, row_spec), check_vma=False)
```

time: 2230 us -> 1210 us (0.54)
  the two profiles are of different devices: /device:TPU:107 before, /device:TPU:97 now
where the time goes in v1:
time: 1210 us
  Pallas kernels  922 us (76%)
  waiting for transfers between devices  117 us (10%)
  matrix products  91.8 us (8%)
  other arithmetic  45.6 us (4%)
  local copies, waits for them, and re-layouts  15.7 us (1%)
  between operations  14.2 us (1%)
    pallas_call x2, Pallas kernels, experts_to_relays(): pl.pallas_call(functools.partial(expert_kernel, group, cap), out_shape=ja...  668 us
    pallas_call x2, Pallas kernels, relay_sums(): pl.pallas_call(functools.partial(relay_kernel, group), out_shape=jax.Shap...  235 us
    all_gather x1, waiting for transfers between devices, device_fn(): gathered_a = lax.all_gather(normed_a, 'ep', tiled=True)  117 us
    sub x2, other arithmetic, attention_block(): attn_prob = jax.nn.softmax(scores, axis=-1).astype(jnp.bfloat16)  34.5 us
    dot_general x2, matrix products, attention_block(): jnp.einsum('qhe,hed->qd', context, w_out, preferred_element_type=jnp.floa...  27.2 us
    dot_general x2, matrix products, attention_block(): jnp.einsum('qhe,khe->hqk', query, keys, preferred_element_type=jnp.float32)  26 us
  transfers between devices with their start and end apart: 3, of which 1 were waited for; matrix products, arithmetic and copies ran while one was open for 13% of the time, Pallas kernels for 41%

profile of v1, /device:TPU:97, one launch (start us, length us, event | category | flops | bytes accessed | tf_op | source)
XLA Modules:
  0.0 1206.9 jit_solution(14351445730628771040)
XLA Ops:
  7.2 0.7 convert_bitcast_fusion
  8.0 0.8 convert_bitcast_fusion.2
  8.7 0.6 pad_maximum_fusion.1
  9.5 0.1 iota_compare_fusion
  9.6 0.7 convert_element_type.97
  10.3 2.1 fusion.30
  12.4 10.0 fusion.18
  22.4 13.2 %fusion.56 = f32[16,512,512]{1,2,0:T(8,128)} fusion(bf16[2048,16,128]{2,1,0:T(8,128)(2,1)} %param.27, bf16[512,16,128]{2,0,1:T(8,128)(2,1)} %fusion.18, bf16[512,2048]{1,0:T(8,128)(2,1)S(1)} %copy-done.2, f32[2048]{0:T(1024)S(1)} %convert_element_type.97, f32[512]{0:T(512)S(1)} %add_rsqrt_fusion.3), kind=kOutput, calls=%fused_computation.68 | convolution fusion | flops 5373952000 | bytes 29370368 | tf_op jit(solution)/shard_map/qhe,khe->hqk/dot_general | solution.py:28
  35.6 17.2 %fusion.80 = (f32[16,512]{1,0:T(8,128)S(1)}, f32[16,512,512]{1,2,0:T(8,128)}) fusion(f32[16,512,512]{1,2,0:T(8,128)} %fusion.56, pred[512,512]{0,1:T(8,128)(4,1)S(1)} %iota_compare_fusion), kind=kOutput, calls=%fused_computation.91 | output fusion | flops 25166336 | bytes 33849344 | tf_op jit(solution)/shard_map/sub | solution.py:31
  52.9 9.3 fusion.22
  62.2 13.6 %fusion.24 = (f32[512]{0:T(512)S(1)}, bf16[512,2048]{1,0:T(8,128)(2,1)S(1)}) fusion(bf16[16,128,2048]{2,1,0:T(8,128)(2,1)} %param.29, f32[16,512,512]{1,2,0:T(8,128)} %get-tuple-element.11, f32[16,512]{1,0:T(8,128)S(1)} %get-tuple-element.10, bf16[512,16,128]{2,0,1:T(8,128)(2,1)} %fusion.22, bf16[512,2048]{1,0:T(8,128)(2,1)} %param.17), kind=kOutput, calls=%fused_computation.40 | convolution fusion | flops 5384437248 | bytes 31492096 | tf_op jit(solution)/shard_map/qhe,hed->qd/dot_general | solution.py:33
  75.8 2.0 fusion.26
  77.9 0.1 all-gather.7.cloned.1.call-start
  78.0 2.1 fusion.34
  80.1 10.0 fusion.20
  90.1 9.3 fusion.16
  99.4 12.8 %fusion.43 = f32[16,512,512]{1,2,0:T(8,128)} fusion(bf16[2048,16,128]{2,1,0:T(8,128)(2,1)} %param.27, bf16[512,16,128]{2,0,1:T(8,128)(2,1)} %fusion.16, bf16[512,2048]{1,0:T(8,128)(2,1)S(1)} %copy-done.3, f32[512]{0:T(512)S(1)} %add_rsqrt_fusion.1, f32[2048]{0:T(1024)S(1)} %convert_element_type.97), kind=kOutput, calls=%fused_computation.63 | convolution fusion | flops 5373952000 | bytes 29370368 | tf_op jit(solution)/shard_map/qhe,khe->hqk/dot_general | solution.py:28
  112.2 17.3 %fusion.81 = (f32[16,512]{1,0:T(8,128)S(1)}, f32[16,512,512]{1,2,0:T(8,128)}) fusion(f32[16,512,512]{1,2,0:T(8,128)} %fusion.43, pred[512,512]{0,1:T(8,128)(4,1)S(1)} %iota_compare_fusion), kind=kOutput, calls=%fused_computation.92 | output fusion | flops 25166336 | bytes 33849344 | tf_op jit(solution)/shard_map/sub | solution.py:31
  129.4 13.6 %fusion.27 = (f32[512]{0:T(512)S(1)}, bf16[512,2048]{1,0:T(8,128)(2,1)S(1)}) fusion(bf16[16,128,2048]{2,1,0:T(8,128)(2,1)} %param.29, f32[16,512,512]{1,2,0:T(8,128)} %get-tuple-element.15, f32[16,512]{1,0:T(8,128)S(1)} %get-tuple-element.14, bf16[512,16,128]{2,0,1:T(8,128)(2,1)} %fusion.20, bf16[512,2048]{1,0:T(8,128)(2,1)} %param.21), kind=kOutput, calls=%fused_computation.43 | convolution fusion | flops 5384437248 | bytes 31492096 | tf_op jit(solution)/shard_map/qhe,hed->qd/dot_general | solution.py:33
  143.0 2.0 fusion.29.after_hbm
  145.2 1.0 dynamic-slice_bitcast_fusion
  146.2 1.0 dynamic-slice_bitcast_fusion.1
  147.2 4.6 copy.38
  151.8 2.3 slice_bitcast_fusion.4
  154.1 6.8 slice_bitcast_fusion
  160.9 117.3 %all-gather.5.cloned.1.call-done.u_hbm = bf16[16384,2048]{1,0:T(8,128)(2,1)} async-done(((bf16[512,2048]{1,0:T(8,128)(2,1)}), bf16[16384,2048]{1,0:T(8,128)(2,1)}) %all-gather.5.cloned.1.call-update) | async-done | bytes 67108880 | tf_op jit(solution)/shard_map/all_gather | solution.py:392
  278.2 369.2 %experts_to_relays.2.ret_hbm = bf16[2,4,8,256,1024]{4,3,2,1,0:T(8,128)(2,1)} custom-call(bf16[16384,2048]{1,0:T(8,128)(2,1)} %all-gather.5.cloned.1.call-done.u_hbm, bf16[512,2048]{1,0:T(8,128)(2,1)} %fusion.29.after_hbm, f32[32,8,512]{2,1,0:T(8,128)} %get-tuple-element.9.dest_ref, bf16[2,2048,1024]{2,1,0:T(8,128)(2,1)} %wg_hbm.3, ...), custom_call_target="tpu_custom_call" | custom-call | flops 120259084288 | bytes 200000000 | tf_op jit(solution)/shard_map/experts_to_relays/pallas_call | solution.py:214
  647.4 117.6 %relay_sums.2.part_ref = f32[2,4,512,1024]{3,2,1,0:T(8,128)} custom-call(bf16[2,4,8,256,1024]{4,3,2,1,0:T(8,128)(2,1)} %experts_to_relays.2.ret_hbm, f32[8,512,8]{2,1,0:T(8,128)} %get-tuple-element.7.dest_ref, f32[8,512,8]{2,1,0:T(8,128)} %get-tuple-element.6.gates_ref), custom_call_target="tpu_custom_call" | custom-call | flops 17179869184 | bytes 50331648 | tf_op jit(solution)/shard_map/relay_sums/pallas_call | solution.py:328
  765.0 9.5 final_sum.2.after_hbm
  774.5 298.5 %experts_to_relays.3.ret_hbm = bf16[2,4,8,256,1024]{4,3,2,1,0:T(8,128)(2,1)} custom-call(bf16[16384,2048]{1,0:T(8,128)(2,1)} %all-gather.7.cloned.1.call-done.u_hbm, bf16[512,2048]{1,0:T(8,128)(2,1)} %final_sum.2.after_hbm, f32[32,8,512]{2,1,0:T(8,128)} %get-tuple-element.8.dest_ref, bf16[2,2048,1024]{2,1,0:T(8,128)(2,1)} %wg_hbm.3, ...), custom_call_target="tpu_custom_call" | custom-call | flops 120259084288 | bytes 200000000 | tf_op jit(solution)/shard_map/experts_to_relays/pallas_call | solution.py:214
  1073.1 117.6 %relay_sums.3.part_ref = f32[2,4,512,1024]{3,2,1,0:T(8,128)} custom-call(bf16[2,4,8,256,1024]{4,3,2,1,0:T(8,128)(2,1)} %experts_to_relays.3.ret_hbm, f32[8,512,8]{2,1,0:T(8,128)} %get-tuple-element.5.dest_ref, f32[8,512,8]{2,1,0:T(8,128)} %get-tuple-element.4.gates_ref), custom_call_target="tpu_custom_call" | custom-call | flops 17179869184 | bytes 50331648 | tf_op jit(solution)/shard_map/relay_sums/pallas_call | solution.py:328
  1190.6 9.5 final_sum.3
  (23 shorter events, 0.4 us)
Async XLA Ops:
  7.2 138.0 %all-gather.9.cloned.1.call-start = ((), (), s32[]{:S(2)}) async-start(), calls=%async_computation.2 | async-start | bytes 2162688 | tf_op jit(solution)/shard_map/all_gather | solution.py:383
  9.4 268.7 %all-gather.5.cloned.1.call-start = ((), (), s32[]{:S(2)}) async-start(), calls=%async_computation | async-start | bytes 69206016 | tf_op jit(solution)/shard_map/all_gather | solution.py:392
  12.4 10.1 copy-start.2
  52.9 9.3 copy-start.4
  75.8 4.2 copy-start
  77.9 696.6 %all-gather.7.cloned.1.call-start = ((), (), s32[]{:S(2)}) async-start(), calls=%async_computation.1 | async-start | bytes 69206016 | tf_op jit(solution)/shard_map/all_gather | solution.py:396
  80.1 10.0 copy-start.3
  143.0 4.2 copy-start.1
Sparse Core Ops, SparseCore 0:
  10.1 42.5 all-gather.8
  78.0 200.1 all-gather.4
  280.3 350.9 all-gather.6

commit v2 on v1

--- a/solution.py
+++ b/solution.py
@@ -11,6 +11,7 @@
 MASK_VALUE = -1e30
 MESH = pl.DeviceIdType.MESH
 VMEM_LIMIT = 64_000_000
+SLOTS_OUT = 4
 
 
 def rms_norm(rows, gain_vec):
@@ -51,6 +52,7 @@
     block_rows = local_experts * cap
     half_dim = model_dim // 2
     steps = group // per_step
+    slots = o_buf.shape[0]
     f_tile = min(512, ffn_dim)
     n_tile = min(512, half_dim)
     side, my_x, my_y, my_core = place(group)
@@ -64,7 +66,7 @@
         if g < 2:
             dx, dy = i, 1 - late
         else:
-            dx, dy = (1 - late) * (side - i) + late * (i + 2), 3 - late
+            dx, dy = i + side // 2, 3 - late
         return lax.rem(my_x + dx, side), lax.rem(my_y + dy, side), g % 2
 
     def load(step, g):
@@ -141,7 +143,7 @@
 
     @pl.loop(0, steps)
     def _(step):
-        slot = lax.rem(step, 2)
+        slot = lax.rem(step, slots)
         for g in range(per_step):
             load(step, g).wait()
             to_x, to_y, core = target(step, g)
@@ -160,9 +162,9 @@
             def _():
                 load(step + 1, g).start()
 
-        @pl.when(step >= 2)
+        @pl.when(step >= slots)
         def _():
-            wait_out(step - 2, slot)
+            wait_out(step - slots, slot)
 
         for e in range(local_experts):
 
@@ -185,8 +187,9 @@
 
         start_out(step, slot)
 
-    for step in range(max(0, steps - 2), steps):
-        wait_out(step, step % 2)
+    @pl.loop(max(0, steps - slots), steps)
+    def _(step):
+        wait_out(step, lax.rem(step, slots))
 
     @pl.loop(1, line)
     def _(k):
@@ -223,10 +226,10 @@
             pltpu.VMEM((per_step, seq_len, model_dim), jnp.bfloat16),
             pltpu.VMEM((local_experts, per_step * cap, model_dim), jnp.bfloat16),
             pltpu.VMEM((per_step * cap, ffn_dim), jnp.bfloat16),
-            pltpu.VMEM((2, 2, per_step, local_experts * cap, model_dim // 2), jnp.bfloat16),
+            pltpu.VMEM((SLOTS_OUT, 2, per_step, local_experts * cap, model_dim // 2), jnp.bfloat16),
             pltpu.SemaphoreType.DMA((3,)),
             pltpu.SemaphoreType.DMA((per_step,)),
-            pltpu.SemaphoreType.DMA((2, 2, per_step)),
+            pltpu.SemaphoreType.DMA((SLOTS_OUT, 2, per_step)),
             pltpu.SemaphoreType.DMA((2, side, 2 * side)),
         ],
         compiler_params=pltpu.CompilerParams(collective_id=0, has_side_effects=True, vmem_limit_bytes=VMEM_LIMIT),

time: 1210 us -> 1160 us (0.959)
  Pallas kernels: 922 us -> 873 us
    pallas_call x2, Pallas kernels: 668 us -> 613 us  [experts_to_relays(): pl.pallas_call(functools.partial(expert_kernel, group, cap), out_shape=ja...]
  transfers between devices with their start and end apart: 3 -> 3, of which waited for: 1 -> 1; matrix products, arithmetic and copies ran while one was open for 13% -> 13% of each run, Pallas kernels for 41% -> 43%
where the time goes in v2:
time: 1160 us
  Pallas kernels  873 us (75%)
  waiting for transfers between devices  117 us (10%)
  matrix products  91.8 us (8%)
  other arithmetic  45.6 us (4%)
  local copies, waits for them, and re-layouts  15.7 us (1%)
  between operations  14.2 us (1%)
    pallas_call x2, Pallas kernels, experts_to_relays(): pl.pallas_call(functools.partial(expert_kernel, group, cap), out_shape=ja...  613 us
    pallas_call x2, Pallas kernels, relay_sums(): pl.pallas_call(functools.partial(relay_kernel, group), out_shape=jax.Shap...  241 us
    all_gather x1, waiting for transfers between devices, device_fn(): gathered_a = lax.all_gather(normed_a, 'ep', tiled=True)  117 us
    sub x2, other arithmetic, attention_block(): attn_prob = jax.nn.softmax(scores, axis=-1).astype(jnp.bfloat16)  34.5 us
    dot_general x2, matrix products, attention_block(): jnp.einsum('qhe,hed->qd', context, w_out, preferred_element_type=jnp.floa...  27.2 us
    dot_general x2, matrix products, attention_block(): jnp.einsum('qhe,khe->hqk', query, keys, preferred_element_type=jnp.float32)  26 us
  transfers between devices with their start and end apart: 3, of which 1 were waited for; matrix products, arithmetic and copies ran while one was open for 13% of the time, Pallas kernels for 43%

profile of v2, /device:TPU:97, one launch (start us, length us, event | category | flops | bytes accessed | tf_op | source)
XLA Modules:
  0.0 1157.8 jit_solution(16588834017937551796)
XLA Ops:
  7.2 0.7 convert_bitcast_fusion
  8.0 0.8 convert_bitcast_fusion.2
  8.7 0.6 pad_maximum_fusion.1
  9.4 0.1 all-gather.5.cloned.1.call-start
  9.5 0.1 iota_compare_fusion
  9.6 0.7 convert_element_type.97
  10.3 2.1 fusion.30
  12.4 10.0 fusion.18
  22.4 13.2 %fusion.56 = f32[16,512,512]{1,2,0:T(8,128)} fusion(bf16[2048,16,128]{2,1,0:T(8,128)(2,1)} %param.27, bf16[512,16,128]{2,0,1:T(8,128)(2,1)} %fusion.18, bf16[512,2048]{1,0:T(8,128)(2,1)S(1)} %copy-done.2, f32[2048]{0:T(1024)S(1)} %convert_element_type.97, f32[512]{0:T(512)S(1)} %add_rsqrt_fusion.3), kind=kOutput, calls=%fused_computation.68 | convolution fusion | flops 5373952000 | bytes 29370368 | tf_op jit(solution)/shard_map/qhe,khe->hqk/dot_general | solution.py:29
  35.6 17.2 %fusion.80 = (f32[16,512]{1,0:T(8,128)S(1)}, f32[16,512,512]{1,2,0:T(8,128)}) fusion(f32[16,512,512]{1,2,0:T(8,128)} %fusion.56, pred[512,512]{0,1:T(8,128)(4,1)S(1)} %iota_compare_fusion), kind=kOutput, calls=%fused_computation.91 | output fusion | flops 25166336 | bytes 33849344 | tf_op jit(solution)/shard_map/sub | solution.py:32
  52.9 9.3 fusion.22
  62.2 13.6 %fusion.24 = (f32[512]{0:T(512)S(1)}, bf16[512,2048]{1,0:T(8,128)(2,1)S(1)}) fusion(bf16[16,128,2048]{2,1,0:T(8,128)(2,1)} %param.29, f32[16,512,512]{1,2,0:T(8,128)} %get-tuple-element.11, f32[16,512]{1,0:T(8,128)S(1)} %get-tuple-element.10, bf16[512,16,128]{2,0,1:T(8,128)(2,1)} %fusion.22, bf16[512,2048]{1,0:T(8,128)(2,1)} %param.17), kind=kOutput, calls=%fused_computation.40 | convolution fusion | flops 5384437248 | bytes 31492096 | tf_op jit(solution)/shard_map/qhe,hed->qd/dot_general | solution.py:34
  75.8 2.0 fusion.26
  78.0 2.1 fusion.34
  80.1 10.0 fusion.20
  90.1 9.3 fusion.16
  99.4 12.8 %fusion.43 = f32[16,512,512]{1,2,0:T(8,128)} fusion(bf16[2048,16,128]{2,1,0:T(8,128)(2,1)} %param.27, bf16[512,16,128]{2,0,1:T(8,128)(2,1)} %fusion.16, bf16[512,2048]{1,0:T(8,128)(2,1)S(1)} %copy-done.3, f32[512]{0:T(512)S(1)} %add_rsqrt_fusion.1, f32[2048]{0:T(1024)S(1)} %convert_element_type.97), kind=kOutput, calls=%fused_computation.63 | convolution fusion | flops 5373952000 | bytes 29370368 | tf_op jit(solution)/shard_map/qhe,khe->hqk/dot_general | solution.py:29
  112.2 17.3 %fusion.81 = (f32[16,512]{1,0:T(8,128)S(1)}, f32[16,512,512]{1,2,0:T(8,128)}) fusion(f32[16,512,512]{1,2,0:T(8,128)} %fusion.43, pred[512,512]{0,1:T(8,128)(4,1)S(1)} %iota_compare_fusion), kind=kOutput, calls=%fused_computation.92 | output fusion | flops 25166336 | bytes 33849344 | tf_op jit(solution)/shard_map/sub | solution.py:32
  129.4 13.6 %fusion.27 = (f32[512]{0:T(512)S(1)}, bf16[512,2048]{1,0:T(8,128)(2,1)S(1)}) fusion(bf16[16,128,2048]{2,1,0:T(8,128)(2,1)} %param.29, f32[16,512,512]{1,2,0:T(8,128)} %get-tuple-element.15, f32[16,512]{1,0:T(8,128)S(1)} %get-tuple-element.14, bf16[512,16,128]{2,0,1:T(8,128)(2,1)} %fusion.20, bf16[512,2048]{1,0:T(8,128)(2,1)} %param.21), kind=kOutput, calls=%fused_computation.43 | convolution fusion | flops 5384437248 | bytes 31492096 | tf_op jit(solution)/shard_map/qhe,hed->qd/dot_general | solution.py:34
  143.0 2.0 fusion.29.after_hbm
  145.2 1.0 dynamic-slice_bitcast_fusion
  146.2 1.0 dynamic-slice_bitcast_fusion.1
  147.2 4.6 copy.38
  151.8 2.3 slice_bitcast_fusion.4
  154.1 6.8 slice_bitcast_fusion
  160.9 117.3 %all-gather.5.cloned.1.call-done.u_hbm = bf16[16384,2048]{1,0:T(8,128)(2,1)} async-done(((bf16[512,2048]{1,0:T(8,128)(2,1)}), bf16[16384,2048]{1,0:T(8,128)(2,1)}) %all-gather.5.cloned.1.call-update) | async-done | bytes 67108880 | tf_op jit(solution)/shard_map/all_gather | solution.py:395
  278.2 364.0 %experts_to_relays.2.ret_hbm = bf16[2,4,8,256,1024]{4,3,2,1,0:T(8,128)(2,1)} custom-call(bf16[16384,2048]{1,0:T(8,128)(2,1)} %all-gather.5.cloned.1.call-done.u_hbm, bf16[512,2048]{1,0:T(8,128)(2,1)} %fusion.29.after_hbm, f32[32,8,512]{2,1,0:T(8,128)} %get-tuple-element.9.dest_ref, bf16[2,2048,1024]{2,1,0:T(8,128)(2,1)} %wg_hbm.3, ...), custom_call_target="tpu_custom_call" | custom-call | flops 120259084288 | bytes 200000000 | tf_op jit(solution)/shard_map/experts_to_relays/pallas_call | solution.py:217
  642.2 119.2 %relay_sums.2.part_ref = f32[2,4,512,1024]{3,2,1,0:T(8,128)} custom-call(bf16[2,4,8,256,1024]{4,3,2,1,0:T(8,128)(2,1)} %experts_to_relays.2.ret_hbm, f32[8,512,8]{2,1,0:T(8,128)} %get-tuple-element.7.dest_ref, f32[8,512,8]{2,1,0:T(8,128)} %get-tuple-element.6.gates_ref), custom_call_target="tpu_custom_call" | custom-call | flops 17179869184 | bytes 50331648 | tf_op jit(solution)/shard_map/relay_sums/pallas_call | solution.py:331
  761.4 9.5 final_sum.2.after_hbm
  770.9 249.1 %experts_to_relays.3.ret_hbm = bf16[2,4,8,256,1024]{4,3,2,1,0:T(8,128)(2,1)} custom-call(bf16[16384,2048]{1,0:T(8,128)(2,1)} %all-gather.7.cloned.1.call-done.u_hbm, bf16[512,2048]{1,0:T(8,128)(2,1)} %final_sum.2.after_hbm, f32[32,8,512]{2,1,0:T(8,128)} %get-tuple-element.8.dest_ref, bf16[2,2048,1024]{2,1,0:T(8,128)(2,1)} %wg_hbm.3, ...), custom_call_target="tpu_custom_call" | custom-call | flops 120259084288 | bytes 200000000 | tf_op jit(solution)/shard_map/experts_to_relays/pallas_call | solution.py:217
  1020.1 121.4 %relay_sums.3.part_ref = f32[2,4,512,1024]{3,2,1,0:T(8,128)} custom-call(bf16[2,4,8,256,1024]{4,3,2,1,0:T(8,128)(2,1)} %experts_to_relays.3.ret_hbm, f32[8,512,8]{2,1,0:T(8,128)} %get-tuple-element.5.dest_ref, f32[8,512,8]{2,1,0:T(8,128)} %get-tuple-element.4.gates_ref), custom_call_target="tpu_custom_call" | custom-call | flops 17179869184 | bytes 50331648 | tf_op jit(solution)/shard_map/relay_sums/pallas_call | solution.py:331
  1141.5 9.5 final_sum.3
  (23 shorter events, 0.4 us)
Async XLA Ops:
  7.2 138.0 %all-gather.9.cloned.1.call-start = ((), (), s32[]{:S(2)}) async-start(), calls=%async_computation.2 | async-start | bytes 2162688 | tf_op jit(solution)/shard_map/all_gather | solution.py:386
  9.4 268.7 %all-gather.5.cloned.1.call-start = ((), (), s32[]{:S(2)}) async-start(), calls=%async_computation | async-start | bytes 69206016 | tf_op jit(solution)/shard_map/all_gather | solution.py:395
  12.4 10.1 copy-start.2
  52.9 9.3 copy-start.4
  75.8 4.2 copy-start
  77.9 693.0 %all-gather.7.cloned.1.call-start = ((), (), s32[]{:S(2)}) async-start(), calls=%async_computation.1 | async-start | bytes 69206016 | tf_op jit(solution)/shard_map/all_gather | solution.py:399
  80.1 10.0 copy-start.3
  143.0 4.2 copy-start.1
Sparse Core Ops, SparseCore 0:
  10.1 42.5 all-gather.8
  78.0 200.1 all-gather.4
  280.3 363.4 all-gather.6
